TPU v7x, 256 devices: a whole 4x4x8 slice. The times are simulated.
256 devices in a mesh: batch: 8 (over y, core), pts: 32 (over z, x).
Axes of the slice: x: 4, y: 4, z: 8, core: 2. Of those that a mesh axis runs over, the one named last changes fastest.
Arguments:
- mesh_attributes: bfloat16 [262144, 512], P(('batch', 'pts')), parts along dimension 0, may hold values from -12 to 12
- occupied_vertices_tally: int32 [256], P(('batch', 'pts')), parts along dimension 0, may hold values from 512 to 1024, as said below
- vertex_content_matrix: bfloat16 [4, 512, 512], replicated, may hold values from -0.25 to 0.25
- vertex_partition_matrix: bfloat16 [4, 512, 512], replicated, may hold values from -0.25 to 0.25
- partition_affinity_matrix: bfloat16 [4, 8, 64, 64], replicated, may hold values from -0.75 to 0.75
- softmax_sharpness: float32 [4, 8], replicated, may hold values from 0.02 to 1
- partition_asking_matrix: bfloat16 [4, 64, 64], replicated, may hold values from -0.75 to 0.75
- partition_matching_matrix: bfloat16 [4, 64, 64], replicated, may hold values from -0.75 to 0.75
- partition_content_matrix: bfloat16 [4, 64, 64], replicated, may hold values from -0.75 to 0.75
- attention_result_matrix: bfloat16 [4, 512, 512], replicated, may hold values from -0.25 to 0.25
- widening_matrix: bfloat16 [4, 512, 512], replicated, may hold values from -0.25 to 0.25
- contracting_matrix: bfloat16 [4, 512, 512], replicated, may hold values from -0.25 to 0.25
Outputs:
- result: bfloat16 [262144, 512], P(('batch', 'pts')), parts along dimension 0
There are 8 independent parts, one for each index of `batch`. A program takes and returns all parts, laid end to end along the dimension named above; an argument that names none is the same for every part. Nothing has to cross between parts.
Inputs may be any that keep to these rules, and one draw needn't show every extreme that they name: `occupied_vertices_tally`: the shard of some index holds 1024 live points in every draw.
All inputs are finite; a program needn't handle non-finite values.
Results may differ from a plain program's by a relative error of at most 0.0055.
Values sent between devices are 32-bit elements; how exact they have to be, the bound alone decides.
No kernel may reach another device: no remote copies, remote signals or barrier semaphores. Data moves between devices by JAX's collectives and lax.ppermute only.
A program may use at most 64 MiB of HBM per device.

v0:
```python
import functools
import jax
import jax.numpy as jnp
from jax import lax
from jax.experimental import pallas as pl
from jax.experimental.pallas import tpu as pltpu
from jax.sharding import PartitionSpec as P

F32 = jnp.float32
BF16 = jnp.bfloat16
TILE = 256
LOG2E = 1.4426950408889634
PAY_ROWS = 288


def dot(a, b, ca=1, cb=0):
    return lax.dot_general(a, b, (((ca,), (cb,)), ((), ())), preferred_element_type=F32)


def split2(x):
    hi = x.astype(BF16)
    lo = (x - hi.astype(F32)).astype(BF16)
    return hi, lo


def dot3(a, b, ca=1, cb=0):
    ah, al = split2(a)
    bh, bl = split2(b)
    return dot(ah, bh, ca, cb) + (dot(ah, bl, ca, cb) + dot(al, bh, ca, cb))


def layer_norm(x):
    c = x - jnp.mean(x, axis=-1, keepdims=True)
    v = jnp.mean(c * c, axis=-1, keepdims=True)
    return c * lax.rsqrt(v + 1e-05)


def same_block(rows, cols, size):
    r = lax.broadcasted_iota(jnp.int32, (rows, cols), 0) // size
    c = lax.broadcasted_iota(jnp.int32, (rows, cols), 1) // size
    return r == c


def pair_diag(w):
    w2 = jnp.concatenate([w, w], axis=1)
    w4 = jnp.concatenate([w2, w2], axis=0)
    return jnp.where(same_block(128, 128, 64), w4, jnp.zeros_like(w4))


def attend(agg, ask, match, content, res_ref, m_ref):
    left = lax.broadcasted_iota(jnp.int32, (64, 128), 1) < 64
    mass = agg[256:264, :].T
    rows = []
    for p in range(4):
        den = jnp.where(left, mass[0:64, p : p + 1], mass[64:128, p : p + 1]) + 1e-05
        rows.append(agg[64 * p : 64 * p + 64, :] / den)
    tokens = jnp.concatenate(rows, axis=0)
    maps = jnp.concatenate([pair_diag(ask), pair_diag(match), pair_diag(content)], axis=1)
    th, tl = split2(tokens)
    qkv = dot(th, maps) + dot(tl, maps)
    keep = same_block(128, 128, 64)
    for p in range(4):
        q = qkv[64 * p : 64 * p + 64, 0:128]
        k = qkv[64 * p : 64 * p + 64, 128:256]
        v = qkv[64 * p : 64 * p + 64, 256:384]
        zero = jnp.zeros_like(q)
        q2 = jnp.concatenate([jnp.where(left, q, zero), jnp.where(left, zero, q)], axis=0)
        scores = dot3(q2, k, 1, 1) * 0.125
        e = jnp.exp(scores - jnp.max(scores, axis=-1, keepdims=True))
        probs = e / jnp.sum(e, axis=-1, keepdims=True)
        att = dot3(probs, v)
        att = jnp.where(keep, att, jnp.zeros_like(att)).astype(BF16)
        m_ref[128 * p : 128 * p + 128, :] = dot(att, res_ref[128 * p : 128 * p + 128, :]).astype(BF16)


def affinity_t(aff, j):
    a = aff[4 * j : 4 * j + 4].reshape(256, 64)
    a4 = jnp.concatenate([a, a, a, a], axis=1)
    a4 = jnp.where(same_block(256, 256, 64), a4, jnp.zeros_like(a4))
    return a4.T


def slice_tile(s, t, tally, coef, v_w, pt_ref, aff_t, w_ref, y_ref, mass_ref):
    n = layer_norm(s).astype(BF16)
    values = dot(n, v_w).astype(BF16)
    ft = dot(pt_ref[...], n, 1, 1).astype(BF16)
    cols = lax.broadcasted_iota(jnp.int32, (1, TILE), 1) + t * TILE
    live = (cols < tally).astype(F32)
    for j in range(2):
        logits = dot(aff_t[j], ft[256 * j : 256 * j + 256, :])
        for i in range(4):
            h = 4 * j + i
            lg = logits[64 * i : 64 * i + 64, :]
            e = jnp.exp2((lg - jnp.max(lg, axis=0, keepdims=True)) * coef[h])
            r = live / jnp.sum(e, axis=0, keepdims=True)
            w = (e * r).astype(BF16)
            w_ref[64 * h : 64 * h + 64, TILE * t : TILE * t + TILE] = w
            wf = w.astype(F32)
            part = wf[:, 0:128]
            for q in range(1, TILE // 128):
                part = part + wf[:, 128 * q : 128 * q + 128]
            if t == 0:
                mass_ref[64 * h : 64 * h + 64, :] = part
            else:
                mass_ref[64 * h : 64 * h + 64, :] += part
        y = dot(
            w_ref[256 * j : 256 * j + 256, TILE * t : TILE * t + TILE],
            values[:, 256 * j : 256 * j + 256],
        )
        if t == 0:
            y_ref[j] = y
        else:
            y_ref[j] += y


def payload(y_ref, mass_ref, pay_ref):
    left = lax.broadcasted_iota(jnp.int32, (64, 128), 1) < 64
    for p in range(4):
        j, q = p // 2, p % 2
        even = y_ref[j, 128 * q : 128 * q + 64, 128 * q : 128 * q + 128]
        odd = y_ref[j, 128 * q + 64 : 128 * q + 128, 128 * q : 128 * q + 128]
        pay_ref[64 * p : 64 * p + 64, :] = jnp.where(left, even, odd)
        row = jnp.sum(mass_ref[128 * p : 128 * p + 128, :].T, axis=0, keepdims=True)
        pay_ref[256 + p : 257 + p, :] = row
    pay_ref[260:PAY_ROWS, :] = jnp.zeros((PAY_ROWS - 260, 128), F32)


def boundary_kernel(layer, first, last, points, *refs):
    refs = list(refs)
    tally_ref, sharp_ref = refs.pop(0), refs.pop(0)
    if not first:
        agg_ref = refs.pop(0)
    s_ref = refs.pop(0)
    if not first:
        w_in_ref = refs.pop(0)
        ask_h, match_h, content_h, res_h, wide_h, narrow_h = refs[:6]
        refs = refs[6:]
    if not last:
        val_h, part_h, aff_h = refs[:3]
        refs = refs[3:]
    if last:
        out_ref = refs.pop(0)
    else:
        if not first:
            s_out_ref = refs.pop(0)
        w_ref, pay_ref = refs.pop(0), refs.pop(0)
    copies = {}

    def fetch(name, src, dst, sem):
        copy = pltpu.make_async_copy(src, dst, sem)
        copy.start()
        copies[name] = copy

    if not first:
        ask_v, match_v, content_v, res_v, wide_v, narrow_v, m_ref, sems_a = refs[:8]
        refs = refs[8:]
        for i, (n, a, b) in enumerate(
            [
                ("ask", ask_h, ask_v),
                ("match", match_h, match_v),
                ("content", content_h, content_v),
                ("res", res_h, res_v),
                ("wide", wide_h, wide_v),
                ("narrow", narrow_h, narrow_v),
            ]
        ):
            fetch(n, a.at[layer - 1], b, sems_a.at[i])
    if not last:
        val_v, part_v, aff_v, pt_ref, y_ref, mass_ref, sems_b = refs
        for i, (n, a, b) in enumerate(
            [("part", part_h, part_v), ("aff", aff_h, aff_v), ("val", val_h, val_v)]
        ):
            fetch(n, a.at[layer], b, sems_b.at[i])
    tally = tally_ref[0]

    if not first:
        for n in ("ask", "match", "content", "res"):
            copies[n].wait()
        attend(agg_ref, ask_v[...], match_v[...], content_v[...], res_v, m_ref)
    if not last:
        copies["part"].wait()
        copies["aff"].wait()
        pt_ref[...] = part_v[...].T
        aff_t = [affinity_t(aff_v[...], 0), affinity_t(aff_v[...], 1)]
        coef = [LOG2E / sharp_ref[layer : layer + 1, h : h + 1] for h in range(8)]
        copies["val"].wait()
    if not first:
        copies["wide"].wait()
        copies["narrow"].wait()

    for t in range(points // TILE):
        at = slice(t * TILE, t * TILE + TILE)
        s = s_ref[at, :].astype(F32)
        if not first:
            s = s + dot(w_in_ref[:, at], m_ref[...], 0, 0)
            n = layer_norm(s).astype(BF16)
            hidden = jax.nn.gelu(dot(n, wide_v[...])).astype(BF16)
            s = s + dot(hidden, narrow_v[...])
        if last:
            rows = lax.broadcasted_iota(jnp.int32, (TILE, 1), 0) + t * TILE
            out_ref[at, :] = jnp.where(rows < tally, s, jnp.zeros_like(s)).astype(BF16)
        else:
            if not first:
                s_out_ref[at, :] = s
            slice_tile(s, t, tally, coef, val_v[...], pt_ref, aff_t, w_ref, y_ref, mass_ref)
    if not last:
        payload(y_ref, mass_ref, pay_ref)


def boundary(layer, layers, tally, sharp, agg, s, w, mats):
    first, last = layer == 0, layer == layers
    points, dim = s.shape
    ask, match, content, res, wide, narrow, val, part, aff = mats
    vmem = pl.BlockSpec(memory_space=pltpu.VMEM)
    smem = pl.BlockSpec(memory_space=pltpu.SMEM)
    hbm = pl.BlockSpec(memory_space=pltpu.HBM)
    args, specs = [tally, sharp], [smem, vmem]
    scratch = []
    sq = (dim, dim)
    if not first:
        args += [agg]
        specs += [vmem]
    args += [s]
    specs += [vmem]
    if not first:
        args += [w, ask, match, content, res, wide, narrow]
        specs += [vmem] + [hbm] * 6
        scratch += [pltpu.VMEM((64, 64), BF16)] * 3 + [pltpu.VMEM(sq, BF16)] * 4
        scratch += [pltpu.SemaphoreType.DMA((6,))]
    if not last:
        args += [val, part, aff]
        specs += [hbm] * 3
        scratch += [
            pltpu.VMEM(sq, BF16),
            pltpu.VMEM(sq, BF16),
            pltpu.VMEM((8, 64, 64), BF16),
            pltpu.VMEM(sq, BF16),
            pltpu.VMEM((2, 256, 256), F32),
            pltpu.VMEM((512, 128), F32),
            pltpu.SemaphoreType.DMA((3,)),
        ]
    if last:
        outs = [jax.ShapeDtypeStruct((points, dim), BF16)]
    else:
        outs = [] if first else [pltpu.VMEM((points, dim), F32)]
        outs += [pltpu.VMEM((dim, points), BF16), pltpu.VMEM((PAY_ROWS, 128), F32)]
    return pl.pallas_call(
        functools.partial(boundary_kernel, layer, first, last, points),
        out_shape=outs,
        in_specs=specs,
        out_specs=[vmem] * len(outs),
        scratch_shapes=scratch,
        compiler_params=pltpu.CompilerParams(vmem_limit_bytes=24 * 1024 * 1024),
        name=f"boundary{layer}",
    )(*args)


def fold_kernel(peers, got_ref, out_ref):
    step = PAY_ROWS // peers
    for r in range(step):
        rows = pl.ds(r, peers, stride=step)
        total = jnp.sum(got_ref[rows, :], axis=0, keepdims=True)
        out_ref[rows, :] = jnp.broadcast_to(total, (peers, 128))


def summed(pay):
    peers = lax.axis_size("pts")
    got = lax.all_to_all(pay.reshape(peers, 1, -1), "pts", 0, 0, tiled=True)
    vmem = pl.BlockSpec(memory_space=pltpu.VMEM)
    own = pl.pallas_call(
        functools.partial(fold_kernel, peers),
        out_shape=pltpu.VMEM((PAY_ROWS, 128), F32),
        in_specs=[vmem],
        out_specs=vmem,
        compiler_params=pltpu.CompilerParams(vmem_limit_bytes=2 * 1024 * 1024),
        name="fold",
    )(got.reshape(PAY_ROWS, 128))
    every = lax.all_to_all(own.reshape(peers, 1, -1), "pts", 0, 0, tiled=True)
    return every.reshape(PAY_ROWS, 128)


def per_device(x, tally, val, part, aff, sharp, ask, match, content, res, wide, narrow):
    mats = (ask, match, content, res, wide, narrow, val, part, aff)
    mats = [pltpu.with_memory_space_constraint(m, pltpu.HBM) for m in mats]
    layers = val.shape[0]
    w, pay = boundary(0, layers, tally, sharp, None, x, None, mats)
    s = x
    for layer in range(1, layers + 1):
        agg = summed(pay)
        got = boundary(layer, layers, tally, sharp, agg, s, w, mats)
        if layer < layers:
            s, w, pay = got
    return got[0]


def solution(mesh):
    placed = (P(("batch", "pts"), None), P(("batch", "pts"))) + (P(),) * 10
    return jax.shard_map(
        per_device, mesh=mesh, in_specs=placed, out_specs=P(("batch", "pts"), None), check_vma=False
    )
```

profile of v0, /device:TPU:16, one launch (start us, length us, event | category | flops | bytes accessed | tf_op | source)
XLA Modules:
  0.0 173.0 jit_solution(17773340375684619840)
XLA Ops:
  0.7 0.0 copy-start
  0.7 1.2 copy-done
  1.9 0.0 copy-start.1
  1.9 0.7 copy-done.1
  2.6 4.9 %boundary0.1 = (bf16[512,1024]{1,0:T(8,128)(2,1)S(1)}, f32[288,128]{1,0:T(8,128)S(1)}) custom-call(s32[1]{0:T(128)S(6)} %copy.21.refs_0_, f32[4,8]{1,0:T(4,128)S(1)} %copy-done.1, bf16[1024,512]{1,0:T(8,128)(2,1)S(1)} %copy-done, bf16[4,512,512]{2,1,0:T(8,128)(2,1)} %refs_11_.5, bf16[4,512,512]{2,1,0:T(8,128)(2,1)} %refs_12_.5, bf16[4,8,64,64]{3,2,1,0:T(8,128)(2,1)} %refs_13_.5), custom_call_target="tpu_custom_call" | custom-call | tf_op jit(solution)/shard_map/boundary0/pallas_call | solution.py:247
  7.4 21.9 %all_to_all.40 = f32[32,1,1152]{2,1,0:T(1,128)S(1)} all-to-all(f32[32,1,1152]{2,1,0:T(1,128)S(1)} %bitcast.31), channel_id=1, replica_groups=mesh['batch'=8,'pts'=32] {'pts'}, dimensions={0} | all-to-all | bytes 294912 | tf_op jit(solution)/shard_map/all_to_all | solution.py:268
  29.3 14.1 %all_to_all.41 = f32[32,1,1152]{2,1,0:T(1,128)S(1)} all-to-all(f32[32,1,1152]{2,1,0:T(1,128)S(1)} %bitcast.17), channel_id=1, replica_groups=mesh['batch'=8,'pts'=32] {'pts'}, dimensions={0} | all-to-all | bytes 294912 | tf_op jit(solution)/shard_map/all_to_all | solution.py:278
  43.4 12.6 %boundary1.1 = (f32[1024,512]{1,0:T(8,128)S(1)}, bf16[512,1024]{1,0:T(8,128)(2,1)S(1)}, f32[288,128]{1,0:T(8,128)S(1)}) custom-call(s32[1]{0:T(128)S(6)} %copy.21.refs_0_, f32[4,8]{1,0:T(4,128)S(1)} %copy-done.1, f32[288,128]{1,0:T(8,128)S(1)} %bitcast.24, bf16[1024,512]{1,0:T(8,128)(2,1)S(1)} %copy-done, bf16[512,1024]{1,0:T(8,128)(2,1)S(1)} %get-tuple-element.17.refs_4_, ...), custom_call_target="tpu_custom_call" | custom-call | tf_op jit(solution)/shard_map/boundary1/pallas_call | solution.py:247
  56.0 13.9 %all_to_all.42 = f32[32,1,1152]{2,1,0:T(1,128)S(1)} all-to-all(f32[32,1,1152]{2,1,0:T(1,128)S(1)} %bitcast.30), channel_id=1, replica_groups=mesh['batch'=8,'pts'=32] {'pts'}, dimensions={0} | all-to-all | bytes 294912 | tf_op jit(solution)/shard_map/all_to_all | solution.py:268
  70.0 13.7 %all_to_all.43 = f32[32,1,1152]{2,1,0:T(1,128)S(1)} all-to-all(f32[32,1,1152]{2,1,0:T(1,128)S(1)} %bitcast.19), channel_id=1, replica_groups=mesh['batch'=8,'pts'=32] {'pts'}, dimensions={0} | all-to-all | bytes 294912 | tf_op jit(solution)/shard_map/all_to_all | solution.py:278
  83.7 12.5 %boundary2.1 = (f32[1024,512]{1,0:T(8,128)S(1)}, bf16[512,1024]{1,0:T(8,128)(2,1)S(1)}, f32[288,128]{1,0:T(8,128)S(1)}) custom-call(s32[1]{0:T(128)S(6)} %copy.21.refs_0_, f32[4,8]{1,0:T(4,128)S(1)} %copy-done.1, f32[288,128]{1,0:T(8,128)S(1)} %bitcast.26, f32[1024,512]{1,0:T(8,128)S(1)} %get-tuple-element.19.refs_3_, ...), custom_call_target="tpu_custom_call" | custom-call | tf_op jit(solution)/shard_map/boundary2/pallas_call | solution.py:247
  96.3 14.0 %all_to_all.44 = f32[32,1,1152]{2,1,0:T(1,128)S(1)} all-to-all(f32[32,1,1152]{2,1,0:T(1,128)S(1)} %bitcast.28), channel_id=1, replica_groups=mesh['batch'=8,'pts'=32] {'pts'}, dimensions={0} | all-to-all | bytes 294912 | tf_op jit(solution)/shard_map/all_to_all | solution.py:268
  110.2 14.0 %all_to_all.45 = f32[32,1,1152]{2,1,0:T(1,128)S(1)} all-to-all(f32[32,1,1152]{2,1,0:T(1,128)S(1)} %bitcast.21), channel_id=1, replica_groups=mesh['batch'=8,'pts'=32] {'pts'}, dimensions={0} | all-to-all | bytes 294912 | tf_op jit(solution)/shard_map/all_to_all | solution.py:278
  124.2 12.5 %boundary3.1 = (f32[1024,512]{1,0:T(8,128)S(1)}, bf16[512,1024]{1,0:T(8,128)(2,1)S(1)}, f32[288,128]{1,0:T(8,128)S(1)}) custom-call(s32[1]{0:T(128)S(6)} %copy.21.refs_0_, f32[4,8]{1,0:T(4,128)S(1)} %copy-done.1, f32[288,128]{1,0:T(8,128)S(1)} %bitcast.27, f32[1024,512]{1,0:T(8,128)S(1)} %get-tuple-element.22.refs_3_, ...), custom_call_target="tpu_custom_call" | custom-call | tf_op jit(solution)/shard_map/boundary3/pallas_call | solution.py:247
  136.7 14.1 %all_to_all.46 = f32[32,1,1152]{2,1,0:T(1,128)S(1)} all-to-all(f32[32,1,1152]{2,1,0:T(1,128)S(1)} %bitcast.29), channel_id=1, replica_groups=mesh['batch'=8,'pts'=32] {'pts'}, dimensions={0} | all-to-all | bytes 294912 | tf_op jit(solution)/shard_map/all_to_all | solution.py:268
  150.8 13.9 %all_to_all.47 = f32[32,1,1152]{2,1,0:T(1,128)S(1)} all-to-all(f32[32,1,1152]{2,1,0:T(1,128)S(1)} %bitcast.23), channel_id=1, replica_groups=mesh['batch'=8,'pts'=32] {'pts'}, dimensions={0} | all-to-all | bytes 294912 | tf_op jit(solution)/shard_map/all_to_all | solution.py:278
  164.7 8.2 %boundary4.1 = bf16[1024,512]{1,0:T(8,128)(2,1)} custom-call(s32[1]{0:T(128)S(6)} %copy.21.refs_0_, f32[4,8]{1,0:T(4,128)S(1)} %copy-done.1, f32[288,128]{1,0:T(8,128)S(1)} %bitcast.25, f32[1024,512]{1,0:T(8,128)S(1)} %get-tuple-element.25.refs_3_, bf16[512,1024]{1,0:T(8,128)(2,1)S(1)} %get-tuple-element.26.refs_4_, bf16[4,64,64]{2,1,0:T(8,128)(2,1)} %refs_5_.9, ...), custom_call_target="tpu_custom_call" | custom-call | tf_op jit(solution)/shard_map/boundary4/pallas_call | solution.py:247
  (4 shorter events, 0.1 us)
Async XLA Ops:
  0.7 1.2 copy-start
  1.9 0.7 copy-start.1
where the time goes:
time: 174 us; the launch traced here: 173 us
  blocking collectives  119 us (68%)
  Pallas kernels  50.7 us (29%)
  local copies, waits for them, and re-layouts  1.9 us (1%)
    all_to_all x4, blocking collectives, summed(): got = lax.all_to_all(pay.reshape(peers, 1, -1), 'pts', 0, 0, tiled=True)  63.8 us
    all_to_all x4, blocking collectives, summed(): every = lax.all_to_all(own.reshape(peers, 1, -1), 'pts', 0, 0, tiled=True)  55.6 us
    pallas_call x5, Pallas kernels, boundary(): pl.pallas_call(functools.partial(boundary_kernel, layer, first, last, poi...  50.7 us

commit v1 on v0

--- a/solution.py
+++ b/solution.py
@@ -8,9 +8,10 @@
 
 F32 = jnp.float32
 BF16 = jnp.bfloat16
-TILE = 256
+TILE = 1024
 LOG2E = 1.4426950408889634
 PAY_ROWS = 288
+VMEM_LIMIT = 16 * 1024 * 1024
 
 
 def dot(a, b, ca=1, cb=0):
@@ -94,23 +95,13 @@
             e = jnp.exp2((lg - jnp.max(lg, axis=0, keepdims=True)) * coef[h])
             r = live / jnp.sum(e, axis=0, keepdims=True)
             w = (e * r).astype(BF16)
-            w_ref[64 * h : 64 * h + 64, TILE * t : TILE * t + TILE] = w
+            w_ref[t, 64 * h : 64 * h + 64, :] = w
             wf = w.astype(F32)
             part = wf[:, 0:128]
             for q in range(1, TILE // 128):
                 part = part + wf[:, 128 * q : 128 * q + 128]
-            if t == 0:
-                mass_ref[64 * h : 64 * h + 64, :] = part
-            else:
-                mass_ref[64 * h : 64 * h + 64, :] += part
-        y = dot(
-            w_ref[256 * j : 256 * j + 256, TILE * t : TILE * t + TILE],
-            values[:, 256 * j : 256 * j + 256],
-        )
-        if t == 0:
-            y_ref[j] = y
-        else:
-            y_ref[j] += y
+            mass_ref[64 * h : 64 * h + 64, :] += part
+        y_ref[j] += dot(w_ref[t, 256 * j : 256 * j + 256, :], values[:, 256 * j : 256 * j + 256])
 
 
 def payload(y_ref, mass_ref, pay_ref):
@@ -127,84 +118,77 @@
 
 def boundary_kernel(layer, first, last, points, *refs):
     refs = list(refs)
-    tally_ref, sharp_ref = refs.pop(0), refs.pop(0)
+    tally_ref = refs.pop(0)
+    tally = tally_ref[0]
+    tiles = points // TILE
+    if first:
+        sharp_h, x_h, val_h, part_h, aff_h, wide_h, narrow_h = refs[:7]
+        sharp_ref, s_ref, aff_ref, wide_ref, narrow_ref, w_ref, pay_ref = refs[7:14]
+        val_ref, part_ref, pt_ref, y_ref, mass_ref, sems = refs[14:]
+        pairs = [
+            (x_h, s_ref),
+            (part_h.at[layer], part_ref),
+            (aff_h, aff_ref),
+            (sharp_h, sharp_ref),
+            (val_h.at[layer], val_ref),
+            (wide_h, wide_ref),
+            (narrow_h, narrow_ref),
+        ]
+        copies = [pltpu.make_async_copy(a, b, sems.at[i]) for i, (a, b) in enumerate(pairs)]
+        for c in copies[:5]:
+            c.start()
+        for c in copies[:5]:
+            c.wait()
+        for c in copies[5:]:
+            c.start()
+        val_at = part_at = ()
+        aff_at = (layer,)
+    else:
+        agg_ref, s_ref, w_in_ref, ask, match, content, res, wide, narrow = refs[:9]
+        refs = refs[9:]
+        if last:
+            out_h, m_ref, out_ref, sems = refs
+        else:
+            sharp_ref, val_ref, part_ref, aff_ref, s_out_ref, w_ref, pay_ref = refs[:7]
+            m_ref, pt_ref, y_ref, mass_ref = refs[7:]
+            val_at = part_at = aff_at = (layer,)
+    if not last:
+        pt_ref[...] = part_ref[part_at + (slice(None), slice(None))].T
+        aff = aff_ref[aff_at + (slice(None), slice(None), slice(None))]
+        aff_t = [affinity_t(aff, 0), affinity_t(aff, 1)]
+        coef = [LOG2E / sharp_ref[layer : layer + 1, h : h + 1] for h in range(8)]
+        y_ref[...] = jnp.zeros_like(y_ref)
+        mass_ref[...] = jnp.zeros_like(mass_ref)
     if not first:
-        agg_ref = refs.pop(0)
-    s_ref = refs.pop(0)
-    if not first:
-        w_in_ref = refs.pop(0)
-        ask_h, match_h, content_h, res_h, wide_h, narrow_h = refs[:6]
-        refs = refs[6:]
-    if not last:
-        val_h, part_h, aff_h = refs[:3]
-        refs = refs[3:]
-    if last:
-        out_ref = refs.pop(0)
-    else:
-        if not first:
-            s_out_ref = refs.pop(0)
-        w_ref, pay_ref = refs.pop(0), refs.pop(0)
-    copies = {}
-
-    def fetch(name, src, dst, sem):
-        copy = pltpu.make_async_copy(src, dst, sem)
-        copy.start()
-        copies[name] = copy
-
-    if not first:
-        ask_v, match_v, content_v, res_v, wide_v, narrow_v, m_ref, sems_a = refs[:8]
-        refs = refs[8:]
-        for i, (n, a, b) in enumerate(
-            [
-                ("ask", ask_h, ask_v),
-                ("match", match_h, match_v),
-                ("content", content_h, content_v),
-                ("res", res_h, res_v),
-                ("wide", wide_h, wide_v),
-                ("narrow", narrow_h, narrow_v),
-            ]
-        ):
-            fetch(n, a.at[layer - 1], b, sems_a.at[i])
-    if not last:
-        val_v, part_v, aff_v, pt_ref, y_ref, mass_ref, sems_b = refs
-        for i, (n, a, b) in enumerate(
-            [("part", part_h, part_v), ("aff", aff_h, aff_v), ("val", val_h, val_v)]
-        ):
-            fetch(n, a.at[layer], b, sems_b.at[i])
-    tally = tally_ref[0]
-
-    if not first:
-        for n in ("ask", "match", "content", "res"):
-            copies[n].wait()
-        attend(agg_ref, ask_v[...], match_v[...], content_v[...], res_v, m_ref)
-    if not last:
-        copies["part"].wait()
-        copies["aff"].wait()
-        pt_ref[...] = part_v[...].T
-        aff_t = [affinity_t(aff_v[...], 0), affinity_t(aff_v[...], 1)]
-        coef = [LOG2E / sharp_ref[layer : layer + 1, h : h + 1] for h in range(8)]
-        copies["val"].wait()
-    if not first:
-        copies["wide"].wait()
-        copies["narrow"].wait()
-
-    for t in range(points // TILE):
+        own = layer - 1
+        attend(agg_ref, ask[own], match[own], content[own], res.at[own], m_ref)
+
+    for t in range(tiles):
         at = slice(t * TILE, t * TILE + TILE)
         s = s_ref[at, :].astype(F32)
         if not first:
-            s = s + dot(w_in_ref[:, at], m_ref[...], 0, 0)
+            s = s + dot(w_in_ref[t], m_ref[...], 0, 0)
             n = layer_norm(s).astype(BF16)
-            hidden = jax.nn.gelu(dot(n, wide_v[...])).astype(BF16)
-            s = s + dot(hidden, narrow_v[...])
+            hidden = jax.nn.gelu(dot(n, wide[own])).astype(BF16)
+            s = s + dot(hidden, narrow[own])
         if last:
             rows = lax.broadcasted_iota(jnp.int32, (TILE, 1), 0) + t * TILE
             out_ref[at, :] = jnp.where(rows < tally, s, jnp.zeros_like(s)).astype(BF16)
+            pltpu.make_async_copy(out_ref.at[at], out_h.at[at], sems.at[t]).start()
         else:
             if not first:
                 s_out_ref[at, :] = s
-            slice_tile(s, t, tally, coef, val_v[...], pt_ref, aff_t, w_ref, y_ref, mass_ref)
-    if not last:
+            val = val_ref[val_at + (slice(None), slice(None))]
+            slice_tile(s, t, tally, coef, val, pt_ref, aff_t, w_ref, y_ref, mass_ref)
+    if last:
+        for t in range(tiles):
+            at = slice(t * TILE, t * TILE + TILE)
+            pltpu.make_async_copy(out_ref.at[at], out_h.at[at], sems.at[t]).wait()
+    else:
         payload(y_ref, mass_ref, pay_ref)
+    if first:
+        for c in copies[5:]:
+            c.wait()
 
 
 def boundary(layer, layers, tally, sharp, agg, s, w, mats):
@@ -214,43 +198,39 @@
     vmem = pl.BlockSpec(memory_space=pltpu.VMEM)
     smem = pl.BlockSpec(memory_space=pltpu.SMEM)
     hbm = pl.BlockSpec(memory_space=pltpu.HBM)
-    args, specs = [tally, sharp], [smem, vmem]
+    args, specs = [tally], [smem]
     scratch = []
     sq = (dim, dim)
-    if not first:
-        args += [agg]
-        specs += [vmem]
-    args += [s]
-    specs += [vmem]
-    if not first:
-        args += [w, ask, match, content, res, wide, narrow]
-        specs += [vmem] + [hbm] * 6
-        scratch += [pltpu.VMEM((64, 64), BF16)] * 3 + [pltpu.VMEM(sq, BF16)] * 4
-        scratch += [pltpu.SemaphoreType.DMA((6,))]
-    if not last:
-        args += [val, part, aff]
-        specs += [hbm] * 3
-        scratch += [
-            pltpu.VMEM(sq, BF16),
-            pltpu.VMEM(sq, BF16),
-            pltpu.VMEM((8, 64, 64), BF16),
-            pltpu.VMEM(sq, BF16),
-            pltpu.VMEM((2, 256, 256), F32),
-            pltpu.VMEM((512, 128), F32),
-            pltpu.SemaphoreType.DMA((3,)),
-        ]
+    sums = [pltpu.VMEM(sq, BF16), pltpu.VMEM((2, 256, 256), F32), pltpu.VMEM((512, 128), F32)]
+    if first:
+        args += [sharp, s, val, part, aff, wide, narrow]
+        specs += [hbm] * 7
+        scratch += [pltpu.VMEM(sq, BF16), pltpu.VMEM(sq, BF16)]
+        scratch += sums + [pltpu.SemaphoreType.DMA((7,))]
+    else:
+        args += [agg, s, w, ask, match, content, res, wide, narrow]
+        specs += [vmem] * 9
+        scratch += [pltpu.VMEM(sq, BF16)]
+        if last:
+            scratch += [pltpu.VMEM(s.shape, BF16), pltpu.SemaphoreType.DMA((points // TILE,))]
+        else:
+            args += [sharp, val, part, aff]
+            specs += [vmem] * 4
+            scratch += sums
     if last:
         outs = [jax.ShapeDtypeStruct((points, dim), BF16)]
     else:
         outs = [] if first else [pltpu.VMEM((points, dim), F32)]
-        outs += [pltpu.VMEM((dim, points), BF16), pltpu.VMEM((PAY_ROWS, 128), F32)]
+        if first:
+            outs = [pltpu.VMEM(m.shape, m.dtype) for m in (sharp, s, aff, wide, narrow)]
+        outs += [pltpu.VMEM((points // TILE, dim, TILE), BF16), pltpu.VMEM((PAY_ROWS, 128), F32)]
     return pl.pallas_call(
         functools.partial(boundary_kernel, layer, first, last, points),
         out_shape=outs,
         in_specs=specs,
-        out_specs=[vmem] * len(outs),
+        out_specs=[hbm if last else vmem] * len(outs),
         scratch_shapes=scratch,
-        compiler_params=pltpu.CompilerParams(vmem_limit_bytes=24 * 1024 * 1024),
+        compiler_params=pltpu.CompilerParams(vmem_limit_bytes=VMEM_LIMIT),
         name=f"boundary{layer}",
     )(*args)
 
@@ -280,14 +260,17 @@
 
 
 def per_device(x, tally, val, part, aff, sharp, ask, match, content, res, wide, narrow):
-    mats = (ask, match, content, res, wide, narrow, val, part, aff)
-    mats = [pltpu.with_memory_space_constraint(m, pltpu.HBM) for m in mats]
+    def placed(space, *arrays):
+        return [pltpu.with_memory_space_constraint(a, space) for a in arrays]
+
     layers = val.shape[0]
-    w, pay = boundary(0, layers, tally, sharp, None, x, None, mats)
-    s = x
+    x, sharp, *far = placed(pltpu.HBM, x, sharp, val, part, aff, wide, narrow)
+    far = [None] * 4 + [far[3], far[4], *far[:3]]
+    sharp, s, aff, wide, narrow, w, pay = boundary(0, layers, tally, sharp, None, x, None, far)
+    near = placed(pltpu.VMEM, ask, match, content, res) + [wide, narrow]
+    near += placed(pltpu.VMEM, val, part) + [aff]
     for layer in range(1, layers + 1):
-        agg = summed(pay)
-        got = boundary(layer, layers, tally, sharp, agg, s, w, mats)
+        got = boundary(layer, layers, tally, sharp, summed(pay), s, w, near)
         if layer < layers:
             s, w, pay = got
     return got[0]

time: 174 us -> 154 us (0.89)
  Pallas kernels: 50.7 us -> 33.5 us
  local copies, waits for them, and re-layouts: 1.9 us -> 0.03 us
    pallas_call x5, Pallas kernels: 50.7 us -> 33.4 us  [boundary(): pl.pallas_call(functools.partial(boundary_kernel, layer, first, last, poi...]
    unnamed x4 -> x12, local copies, waits for them, and re-layouts: 1.9 us -> 0.03 us
where the time goes in v1:
time: 154 us
  blocking collectives  119 us (77%)
  Pallas kernels  33.5 us (22%)
    all_to_all x4, blocking collectives, summed(): got = lax.all_to_all(pay.reshape(peers, 1, -1), 'pts', 0, 0, tiled=True)  63.7 us
    all_to_all x4, blocking collectives, summed(): every = lax.all_to_all(own.reshape(peers, 1, -1), 'pts', 0, 0, tiled=True)  55.7 us
    pallas_call x5, Pallas kernels, boundary(): pl.pallas_call(functools.partial(boundary_kernel, layer, first, last, poi...  33.4 us

profile of v1, /device:TPU:16, one launch (start us, length us, event | category | flops | bytes accessed | tf_op | source)
XLA Modules:
  0.0 153.9 jit_solution(15070250456127360976)
XLA Ops:
  0.7 0.0 copy-start
  0.7 0.0 copy-start.1
  0.7 0.0 copy-start.2
  0.7 0.0 copy-start.3
  0.7 0.0 copy-start.4
  0.7 0.0 copy-start.5
  0.7 5.4 %boundary0.1 = (f32[4,8]{1,0:T(4,128)S(1)}, bf16[1024,512]{1,0:T(8,128)(2,1)S(1)}, bf16[4,8,64,64]{3,2,1,0:T(8,128)(2,1)S(1)}, bf16[4,512,512]{2,1,0:T(8,128)(2,...) custom-call(s32[1]{0:T(128)S(6)} %copy.21.refs_0_, ...), custom_call_target="tpu_custom_call" | custom-call | tf_op jit(solution)/shard_map/boundary0/pallas_call | solution.py:227
  6.1 21.9 %all_to_all.40 = f32[32,1,1152]{2,1,0:T(1,128)S(1)} all-to-all(f32[32,1,1152]{2,1,0:T(1,128)S(1)} %bitcast.29), channel_id=1, replica_groups=mesh['batch'=8,'pts'=32] {'pts'}, dimensions={0} | all-to-all | bytes 294912 | tf_op jit(solution)/shard_map/all_to_all | solution.py:248
  28.0 14.1 %all_to_all.41 = f32[32,1,1152]{2,1,0:T(1,128)S(1)} all-to-all(f32[32,1,1152]{2,1,0:T(1,128)S(1)} %bitcast.17), channel_id=1, replica_groups=mesh['batch'=8,'pts'=32] {'pts'}, dimensions={0} | all-to-all | bytes 294912 | tf_op jit(solution)/shard_map/all_to_all | solution.py:258
  42.1 0.0 copy-done
  42.1 0.0 copy-done.1
  42.1 0.0 copy-done.2
  42.1 0.0 copy-done.3
  42.1 0.0 copy-done.4
  42.2 0.0 copy-done.5
  42.2 7.4 %boundary1.1 = (f32[1024,512]{1,0:T(8,128)S(1)}, bf16[1,512,1024]{2,1,0:T(8,128)(2,1)S(1)}, f32[288,128]{1,0:T(8,128)S(1)}) custom-call(s32[1]{0:T(128)S(6)} %copy.21.refs_0_, f32[288,128]{1,0:T(8,128)S(1)} %bitcast.24, bf16[1024,512]{1,0:T(8,128)(2,1)S(1)} %get-tuple-element.22.refs_2_, bf16[1,512,1024]{2,1,0:T(8,128)(2,1)S(1)} %get-tuple-element.23.refs_3_, ...), custom_call_target="tpu_custom_call" | custom-call | tf_op jit(solution)/shard_map/boundary1/pallas_call | solution.py:227
  49.6 13.9 %all_to_all.42 = f32[32,1,1152]{2,1,0:T(1,128)S(1)} all-to-all(f32[32,1,1152]{2,1,0:T(1,128)S(1)} %bitcast.30), channel_id=1, replica_groups=mesh['batch'=8,'pts'=32] {'pts'}, dimensions={0} | all-to-all | bytes 294912 | tf_op jit(solution)/shard_map/all_to_all | solution.py:248
  63.5 13.7 %all_to_all.43 = f32[32,1,1152]{2,1,0:T(1,128)S(1)} all-to-all(f32[32,1,1152]{2,1,0:T(1,128)S(1)} %bitcast.19), channel_id=1, replica_groups=mesh['batch'=8,'pts'=32] {'pts'}, dimensions={0} | all-to-all | bytes 294912 | tf_op jit(solution)/shard_map/all_to_all | solution.py:258
  77.3 7.4 %boundary2.1 = (f32[1024,512]{1,0:T(8,128)S(1)}, bf16[1,512,1024]{2,1,0:T(8,128)(2,1)S(1)}, f32[288,128]{1,0:T(8,128)S(1)}) custom-call(s32[1]{0:T(128)S(6)} %copy.21.refs_0_, f32[288,128]{1,0:T(8,128)S(1)} %bitcast.27, f32[1024,512]{1,0:T(8,128)S(1)} %get-tuple-element.29.refs_2_, bf16[1,512,1024]{2,1,0:T(8,128)(2,1)S(1)} %get-tuple-element.30.refs_3_, ...), custom_call_target="tpu_custom_call" | custom-call | tf_op jit(solution)/shard_map/boundary2/pallas_call | solution.py:227
  84.7 14.0 %all_to_all.44 = f32[32,1,1152]{2,1,0:T(1,128)S(1)} all-to-all(f32[32,1,1152]{2,1,0:T(1,128)S(1)} %bitcast.31), channel_id=1, replica_groups=mesh['batch'=8,'pts'=32] {'pts'}, dimensions={0} | all-to-all | bytes 294912 | tf_op jit(solution)/shard_map/all_to_all | solution.py:248
  98.7 14.0 %all_to_all.45 = f32[32,1,1152]{2,1,0:T(1,128)S(1)} all-to-all(f32[32,1,1152]{2,1,0:T(1,128)S(1)} %bitcast.21), channel_id=1, replica_groups=mesh['batch'=8,'pts'=32] {'pts'}, dimensions={0} | all-to-all | bytes 294912 | tf_op jit(solution)/shard_map/all_to_all | solution.py:258
  112.7 7.4 %boundary3.1 = (f32[1024,512]{1,0:T(8,128)S(1)}, bf16[1,512,1024]{2,1,0:T(8,128)(2,1)S(1)}, f32[288,128]{1,0:T(8,128)S(1)}) custom-call(s32[1]{0:T(128)S(6)} %copy.21.refs_0_, f32[288,128]{1,0:T(8,128)S(1)} %bitcast.26, f32[1024,512]{1,0:T(8,128)S(1)} %get-tuple-element.32.refs_2_, bf16[1,512,1024]{2,1,0:T(8,128)(2,1)S(1)} %get-tuple-element.33.refs_3_, ...), custom_call_target="tpu_custom_call" | custom-call | tf_op jit(solution)/shard_map/boundary3/pallas_call | solution.py:227
  120.1 14.0 %all_to_all.46 = f32[32,1,1152]{2,1,0:T(1,128)S(1)} all-to-all(f32[32,1,1152]{2,1,0:T(1,128)S(1)} %bitcast.28), channel_id=1, replica_groups=mesh['batch'=8,'pts'=32] {'pts'}, dimensions={0} | all-to-all | bytes 294912 | tf_op jit(solution)/shard_map/all_to_all | solution.py:248
  134.1 14.0 %all_to_all.47 = f32[32,1,1152]{2,1,0:T(1,128)S(1)} all-to-all(f32[32,1,1152]{2,1,0:T(1,128)S(1)} %bitcast.23), channel_id=1, replica_groups=mesh['batch'=8,'pts'=32] {'pts'}, dimensions={0} | all-to-all | bytes 294912 | tf_op jit(solution)/shard_map/all_to_all | solution.py:258
  148.0 5.7 %boundary4.1 = bf16[1024,512]{1,0:T(8,128)(2,1)} custom-call(s32[1]{0:T(128)S(6)} %copy.21.refs_0_, f32[288,128]{1,0:T(8,128)S(1)} %bitcast.25, f32[1024,512]{1,0:T(8,128)S(1)} %get-tuple-element.35.refs_2_, bf16[1,512,1024]{2,1,0:T(8,128)(2,1)S(1)} %get-tuple-element.36.refs_3_, bf16[4,64,64]{2,1,0:T(8,128)(2,1)S(1)} %copy-done.3, ...), custom_call_target="tpu_custom_call" | custom-call | tf_op jit(solution)/shard_map/boundary4/pallas_call | solution.py:227
  (4 shorter events, 0.1 us)
Async XLA Ops:
  0.7 41.5 %copy-start = (bf16[4,512,512]{2,1,0:T(8,128)(2,1)S(1)}, bf16[4,512,512]{2,1,0:T(8,128)(2,1)}, u32[]{:S(2)}) copy-start(bf16[4,512,512]{2,1,0:T(8,128)(2,1)} %refs_11_.5) | copy-start | bytes 6291460
  0.7 41.5 %copy-start.1 = (bf16[4,512,512]{2,1,0:T(8,128)(2,1)S(1)}, bf16[4,512,512]{2,1,0:T(8,128)(2,1)}, u32[]{:S(2)}) copy-start(bf16[4,512,512]{2,1,0:T(8,128)(2,1)} %refs_12_.5) | copy-start | bytes 6291460
  0.7 41.5 %copy-start.2 = (bf16[4,512,512]{2,1,0:T(8,128)(2,1)S(1)}, bf16[4,512,512]{2,1,0:T(8,128)(2,1)}, u32[]{:S(2)}) copy-start(bf16[4,512,512]{2,1,0:T(8,128)(2,1)} %refs_7_.9) | copy-start | bytes 6291460
  0.7 41.5 %copy-start.3 = (bf16[4,64,64]{2,1,0:T(8,128)(2,1)S(1)}, bf16[4,64,64]{2,1,0:T(8,128)(2,1)}, u32[]{:S(2)}) copy-start(bf16[4,64,64]{2,1,0:T(8,128)(2,1)} %refs_4_.9) | copy-start | bytes 98308
  0.7 41.5 %copy-start.4 = (bf16[4,64,64]{2,1,0:T(8,128)(2,1)S(1)}, bf16[4,64,64]{2,1,0:T(8,128)(2,1)}, u32[]{:S(2)}) copy-start(bf16[4,64,64]{2,1,0:T(8,128)(2,1)} %refs_5_.9) | copy-start | bytes 98308
  0.7 41.5 %copy-start.5 = (bf16[4,64,64]{2,1,0:T(8,128)(2,1)S(1)}, bf16[4,64,64]{2,1,0:T(8,128)(2,1)}, u32[]{:S(2)}) copy-start(bf16[4,64,64]{2,1,0:T(8,128)(2,1)} %refs_6_.9) | copy-start | bytes 98308

commit v2 on v1

v2 whole, which is shorter than its diff:
```python
import functools
import jax
import jax.numpy as jnp
from jax import lax
from jax.experimental import pallas as pl
from jax.experimental.pallas import tpu as pltpu
from jax.sharding import PartitionSpec as P

F32 = jnp.float32
BF16 = jnp.bfloat16
SLAB = 256
TILES = (1024, 512, 512)
LAG = 1
LOG2E = 1.4426950408889634
PAY_ROWS = 288
VMEM_LIMIT = 16 * 1024 * 1024


def dot(a, b, ca=1, cb=0):
    return lax.dot_general(a, b, (((ca,), (cb,)), ((), ())), preferred_element_type=F32)


def split2(x):
    hi = x.astype(BF16)
    lo = (x - hi.astype(F32)).astype(BF16)
    return hi, lo


def dot3(a, b, ca=1, cb=0):
    ah, al = split2(a)
    bh, bl = split2(b)
    return dot(ah, bh, ca, cb) + (dot(ah, bl, ca, cb) + dot(al, bh, ca, cb))


def layer_norm(x):
    c = x - jnp.mean(x, axis=-1, keepdims=True)
    v = jnp.mean(c * c, axis=-1, keepdims=True)
    return c * lax.rsqrt(v + 1e-05)


def same_block(rows, cols, size):
    r = lax.broadcasted_iota(jnp.int32, (rows, cols), 0) // size
    c = lax.broadcasted_iota(jnp.int32, (rows, cols), 1) // size
    return r == c


def pair_diag(w):
    w2 = jnp.concatenate([w, w], axis=1)
    w4 = jnp.concatenate([w2, w2], axis=0)
    return jnp.where(same_block(128, 128, 64), w4, jnp.zeros_like(w4))


def attend(agg, ask, match, content, res_ref, m_ref):
    keep = same_block(128, 128, 64)
    inverse = 1.0 / (agg[256:264, :] + 1e-05)
    inverse_t = inverse.T
    maps = jnp.concatenate([pair_diag(ask), pair_diag(match), pair_diag(content)], axis=1)
    th, tl = split2(agg[0:256, :])
    qkv = dot(jnp.concatenate([th, tl], axis=1), jnp.concatenate([maps, maps], axis=0))

    def spread_out(p, at):
        x = qkv[64 * p : 64 * p + 64, 128 * at : 128 * at + 128]
        x2 = jnp.concatenate([x, x], axis=0)
        return jnp.where(keep, x2, jnp.zeros_like(x2))

    pairs = range(4)
    scores = []
    for p in pairs:
        qh, ql = split2(spread_out(p, 0))
        kh, kl = split2(spread_out(p, 1))
        q3 = jnp.concatenate([qh, ql, qh], axis=1)
        k3 = jnp.concatenate([kh, kh, kl], axis=1)
        scores.append(dot(q3, k3, 1, 1))
    vr = [
        dot(spread_out(p, 2).astype(BF16), res_ref[128 * p : 128 * p + 128, :]).astype(BF16)
        for p in pairs
    ]
    scores = [
        scores[p] * inverse_t[:, p : p + 1] * (inverse[p : p + 1, :] * 0.125) for p in pairs
    ]
    scores = [jnp.where(keep, x, jnp.full_like(x, -1e30)) for x in scores]
    tops = [jnp.max(x, axis=-1, keepdims=True) for x in scores]
    scores = [jnp.exp(scores[p] - tops[p]) for p in pairs]
    sums = [jnp.sum(x, axis=-1, keepdims=True) for x in scores]
    for p in pairs:
        probs = scores[p] * (1.0 / sums[p]) * inverse[p : p + 1, :]
        m_ref[128 * p : 128 * p + 128, :] = dot(probs.astype(BF16), vr[p]).astype(BF16)


def slice_map(part_ref, aff, coef, pt_ref):
    for j in range(2):
        a = aff[4 * j : 4 * j + 4].reshape(256, 64)
        a4 = jnp.concatenate([a, a, a, a], axis=1)
        a4 = jnp.where(same_block(256, 256, 64), a4, jnp.zeros_like(a4))
        both = dot(a4, part_ref[:, 256 * j : 256 * j + 256], 0, 1)
        for i in range(4):
            h = 4 * j + i
            rows = both[64 * i : 64 * i + 64, :] * coef[h]
            pt_ref[64 * h : 64 * h + 64, :] = rows.astype(BF16)


def gelu_twice(x):
    inner = x * (0.7978845608028654 + 0.03567740813636141 * (x * x))
    return x + x * jnp.tanh(inner)


def tile_stages(t, cfg):
    size = cfg["size"]
    at = slice(t * size, t * size + size)
    slabs = range(t * size // SLAB, (t + 1) * size // SLAB)
    live = {}

    def joined(name, rows):
        return jnp.concatenate([cfg[name][i, rows, :] for i in slabs], axis=1)

    def start():
        live["s"] = cfg["s"][at, :].astype(F32)
        if not cfg["first"]:
            live["s"] = live["s"] + dot(joined("w_in", slice(None)), cfg["m"][...], 0, 0)

    def norm():
        live["n"] = layer_norm(live["s"]).astype(BF16)

    def widen():
        live["g"] = gelu_twice(dot(live["n"], cfg["wide"][...])).astype(BF16)

    def contract():
        live["s"] = live["s"] + dot(live["g"], cfg["narrow"][...])

    def finish():
        rows = lax.broadcasted_iota(jnp.int32, (size, 1), 0) + t * size
        s = live["s"]
        cfg["out"][at, :] = jnp.where(rows < cfg["tally"], s, jnp.zeros_like(s)).astype(BF16)
        pltpu.make_async_copy(cfg["out"].at[at], cfg["out_h"].at[at], cfg["sems"].at[t]).start()

    def keep():
        cfg["s_out"][at, :] = live["s"]

    def project():
        live["v"] = dot(live["n"], cfg["val"][...]).astype(BF16)
        live["l"] = dot(cfg["pt"][...], live["n"], 1, 1)

    def weigh():
        cols = lax.broadcasted_iota(jnp.int32, (1, size), 1) + t * size
        on = (cols < cfg["tally"]).astype(F32)
        for h in range(8):
            lg = live["l"][64 * h : 64 * h + 64, :]
            e = jnp.exp2(lg - jnp.max(lg, axis=0, keepdims=True))
            w = e * (on / jnp.sum(e, axis=0, keepdims=True))
            for q, i in enumerate(slabs):
                slab = w[:, SLAB * q : SLAB * q + SLAB]
                cfg["w"][i, 64 * h : 64 * h + 64, :] = slab.astype(BF16)
            part = w[:, 0:128]
            for q in range(1, size // 128):
                part = part + w[:, 128 * q : 128 * q + 128]
            if t == 0:
                cfg["mass"][64 * h : 64 * h + 64, :] = part
            else:
                cfg["mass"][64 * h : 64 * h + 64, :] += part

    def gather():
        for j in range(2):
            part = slice(256 * j, 256 * j + 256)
            y = dot(joined("w", part), live["v"][:, part])
            if t == 0:
                cfg["y"][j] = y
            else:
                cfg["y"][j] += y

    steps = [start]
    if not cfg["first"]:
        steps += [norm, widen, contract]
    if cfg["last"]:
        return steps + [finish]
    if not cfg["first"]:
        steps += [keep]
    return steps + [norm, project, weigh, gather]


def payload(y_ref, mass_ref, pay_ref):
    left = lax.broadcasted_iota(jnp.int32, (64, 128), 1) < 64
    for p in range(4):
        j, q = p // 2, p % 2
        even = y_ref[j, 128 * q : 128 * q + 64, 128 * q : 128 * q + 128]
        odd = y_ref[j, 128 * q + 64 : 128 * q + 128, 128 * q : 128 * q + 128]
        pay_ref[64 * p : 64 * p + 64, :] = jnp.where(left, even, odd)
        row = jnp.sum(mass_ref[128 * p : 128 * p + 128, :].T, axis=0, keepdims=True)
        pay_ref[256 + p : 257 + p, :] = row
    pay_ref[260:PAY_ROWS, :] = jnp.zeros((PAY_ROWS - 260, 128), F32)


def boundary_kernel(layer, first, last, points, *refs):
    refs = list(refs)
    tally_ref = refs.pop(0)
    tally = tally_ref[0]
    size = TILES[0 if first else 2 if last else 1]
    tiles = points // size
    if first:
        sharp_h, x_h, val_h, part_h, aff_h, wide_h, narrow_h = refs[:7]
        sharp_ref, s_ref, aff_ref, wide_ref, narrow_ref, w_ref, pay_ref = refs[7:14]
        val_ref, part_ref, pt_ref, y_ref, mass_ref, sems = refs[14:]
        pairs = [
            (sharp_h, sharp_ref),
            (aff_h, aff_ref),
            (part_h.at[layer], part_ref),
            (x_h, s_ref),
            (val_h.at[layer], val_ref),
            (wide_h, wide_ref),
            (narrow_h, narrow_ref),
        ]
        copies = [pltpu.make_async_copy(a, b, sems.at[i]) for i, (a, b) in enumerate(pairs)]
        for c in copies:
            c.start()
        val_at = part_at = None
        aff_at = layer
    else:
        agg_ref, s_ref, w_in_ref, ask, match, content, res, wide, narrow = refs[:9]
        refs = refs[9:]
        if last:
            out_h, m_ref, half_ref, out_ref, sems = refs
        else:
            sharp_ref, val_ref, part_ref, aff_ref, s_out_ref, w_ref, pay_ref = refs[:7]
            m_ref, half_ref, pt_ref, y_ref, mass_ref = refs[7:]
            val_at = part_at = aff_at = layer
    cfg = dict(size=size, first=first, last=last, tally=tally, s=s_ref)
    if first:
        for c in copies[:3]:
            c.wait()
    if not last:
        coef = [LOG2E / sharp_ref[layer : layer + 1, h : h + 1] for h in range(8)]
        slice_map(part_ref.at[part_at] if part_at is not None else part_ref, aff_ref[aff_at], coef, pt_ref)
        val = val_ref.at[val_at] if val_at is not None else val_ref
        cfg.update(val=val, pt=pt_ref, w=w_ref, y=y_ref, mass=mass_ref)
    if first:
        for c in copies[3:5]:
            c.wait()
    else:
        own = layer - 1
        half_ref[...] = narrow[own] * 0.5
        attend(agg_ref, ask[own], match[own], content[own], res.at[own], m_ref)
        cfg.update(w_in=w_in_ref, m=m_ref, wide=wide.at[own], narrow=half_ref)
        if last:
            cfg.update(out=out_ref, out_h=out_h, sems=sems)
        else:
            cfg.update(s_out=s_out_ref)

    lists = [tile_stages(t, cfg) for t in range(tiles)]
    count = len(lists[0])
    for k in range(count + LAG * (tiles - 1)):
        for t in range(tiles):
            if 0 <= k - LAG * t < count:
                lists[t][k - LAG * t]()
    if last:
        for t in range(tiles):
            at = slice(t * size, t * size + size)
            pltpu.make_async_copy(out_ref.at[at], out_h.at[at], sems.at[t]).wait()
    else:
        payload(y_ref, mass_ref, pay_ref)
    if first:
        for c in copies[5:]:
            c.wait()


def boundary(layer, layers, tally, sharp, agg, s, w, mats):
    first, last = layer == 0, layer == layers
    points, dim = s.shape
    ask, match, content, res, wide, narrow, val, part, aff = mats
    vmem = pl.BlockSpec(memory_space=pltpu.VMEM)
    smem = pl.BlockSpec(memory_space=pltpu.SMEM)
    hbm = pl.BlockSpec(memory_space=pltpu.HBM)
    args, specs = [tally], [smem]
    scratch = []
    sq = (dim, dim)
    sums = [pltpu.VMEM(sq, BF16), pltpu.VMEM((2, 256, 256), F32), pltpu.VMEM((512, 128), F32)]
    if first:
        args += [sharp, s, val, part, aff, wide, narrow]
        specs += [hbm] * 7
        scratch += [pltpu.VMEM(sq, BF16), pltpu.VMEM(sq, BF16)]
        scratch += sums + [pltpu.SemaphoreType.DMA((7,))]
    else:
        args += [agg, s, w, ask, match, content, res, wide, narrow]
        specs += [vmem] * 9
        scratch += [pltpu.VMEM(sq, BF16)] * 2
        if last:
            scratch += [pltpu.VMEM(s.shape, BF16), pltpu.SemaphoreType.DMA((points // TILES[2],))]
        else:
            args += [sharp, val, part, aff]
            specs += [vmem] * 4
            scratch += sums
    if last:
        outs = [jax.ShapeDtypeStruct((points, dim), BF16)]
    else:
        outs = [] if first else [pltpu.VMEM((points, dim), F32)]
        if first:
            outs = [pltpu.VMEM(m.shape, m.dtype) for m in (sharp, s, aff, wide, narrow)]
        outs += [pltpu.VMEM((points // SLAB, dim, SLAB), BF16), pltpu.VMEM((PAY_ROWS, 128), F32)]
    return pl.pallas_call(
        functools.partial(boundary_kernel, layer, first, last, points),
        out_shape=outs,
        in_specs=specs,
        out_specs=[hbm if last else vmem] * len(outs),
        scratch_shapes=scratch,
        compiler_params=pltpu.CompilerParams(vmem_limit_bytes=VMEM_LIMIT),
        name=f"boundary{layer}",
    )(*args)


def fold_kernel(peers, got_ref, out_ref):
    step = PAY_ROWS // peers
    for r in range(step):
        rows = pl.ds(r, peers, stride=step)
        total = jnp.sum(got_ref[rows, :], axis=0, keepdims=True)
        out_ref[rows, :] = jnp.broadcast_to(total, (peers, 128))


def summed(pay):
    peers = lax.axis_size("pts")
    got = lax.all_to_all(pay.reshape(peers, 1, -1), "pts", 0, 0, tiled=True)
    vmem = pl.BlockSpec(memory_space=pltpu.VMEM)
    own = pl.pallas_call(
        functools.partial(fold_kernel, peers),
        out_shape=pltpu.VMEM((PAY_ROWS, 128), F32),
        in_specs=[vmem],
        out_specs=vmem,
        compiler_params=pltpu.CompilerParams(vmem_limit_bytes=2 * 1024 * 1024),
        name="fold",
    )(got.reshape(PAY_ROWS, 128))
    every = lax.all_to_all(own.reshape(peers, 1, -1), "pts", 0, 0, tiled=True)
    return every.reshape(PAY_ROWS, 128)


def per_device(x, tally, val, part, aff, sharp, ask, match, content, res, wide, narrow):
    def placed(space, *arrays):
        return [pltpu.with_memory_space_constraint(a, space) for a in arrays]

    layers = val.shape[0]
    x, sharp, *far = placed(pltpu.HBM, x, sharp, val, part, aff, wide, narrow)
    far = [None] * 4 + [far[3], far[4], *far[:3]]
    sharp, s, aff, wide, narrow, w, pay = boundary(0, layers, tally, sharp, None, x, None, far)
    pay, *later = lax.optimization_barrier((pay, ask, match, content, res, val, part))
    later = placed(pltpu.VMEM, *later)
    near = later[:4] + [wide, narrow] + later[4:] + [aff]
    for layer in range(1, layers + 1):
        got = boundary(layer, layers, tally, sharp, summed(pay), s, w, near)
        if layer < layers:
            s, w, pay = got
    return got[0]


def solution(mesh):
    placed = (P(("batch", "pts"), None), P(("batch", "pts"))) + (P(),) * 10
    return jax.shard_map(
        per_device, mesh=mesh, in_specs=placed, out_specs=P(("batch", "pts"), None), check_vma=False
    )
```

time: 154 us -> 146 us (0.948)
  Pallas kernels: 33.5 us -> 24.7 us
    pallas_call x5, Pallas kernels: 33.4 us -> 24.6 us  [boundary(): pl.pallas_call(functools.partial(boundary_kernel, layer, first, last, poi...]
where the time goes in v2:
time: 146 us; the launch traced here: 145 us
  blocking collectives  119 us (82%)
  Pallas kernels  24.7 us (17%)
    all_to_all x4, blocking collectives, summed(): got = lax.all_to_all(pay.reshape(peers, 1, -1), 'pts', 0, 0, tiled=True)  63.9 us
    all_to_all x4, blocking collectives, summed(): every = lax.all_to_all(own.reshape(peers, 1, -1), 'pts', 0, 0, tiled=True)  55.6 us
    pallas_call x5, Pallas kernels, boundary(): pl.pallas_call(functools.partial(boundary_kernel, layer, first, last, poi...  24.6 us

profile of v2, /device:TPU:16, one launch (start us, length us, event | category | flops | bytes accessed | tf_op | source)
XLA Modules:
  0.0 145.1 jit_solution(12748698658007626764)
XLA Ops:
  0.7 0.0 copy-start
  0.7 0.0 copy-start.1
  0.7 0.0 copy-start.2
  0.7 0.0 copy-start.3
  0.7 0.0 copy-start.4
  0.7 0.0 copy-start.5
  0.7 4.5 %boundary0.1 = (f32[4,8]{1,0:T(4,128)S(1)}, bf16[1024,512]{1,0:T(8,128)(2,1)S(1)}, bf16[4,8,64,64]{3,2,1,0:T(8,128)(2,1)S(1)}, bf16[4,512,512]{2,1,0:T(8,128)(2,...) custom-call(s32[1]{0:T(128)S(6)} %copy.21.refs_0_, ...), custom_call_target="tpu_custom_call" | custom-call | tf_op jit(solution)/shard_map/boundary0/pallas_call | solution.py:297
  5.2 21.9 %all_to_all.40 = f32[32,1,1152]{2,1,0:T(1,128)S(1)} all-to-all(f32[32,1,1152]{2,1,0:T(1,128)S(1)} %bitcast.29), channel_id=1, replica_groups=mesh['batch'=8,'pts'=32] {'pts'}, dimensions={0} | all-to-all | bytes 294912 | tf_op jit(solution)/shard_map/all_to_all | solution.py:318
  27.1 14.1 %all_to_all.41 = f32[32,1,1152]{2,1,0:T(1,128)S(1)} all-to-all(f32[32,1,1152]{2,1,0:T(1,128)S(1)} %bitcast.17), channel_id=1, replica_groups=mesh['batch'=8,'pts'=32] {'pts'}, dimensions={0} | all-to-all | bytes 294912 | tf_op jit(solution)/shard_map/all_to_all | solution.py:328
  41.2 0.0 copy-done
  41.2 0.0 copy-done.1
  41.2 0.0 copy-done.2
  41.2 0.0 copy-done.3
  41.2 0.0 copy-done.4
  41.2 0.0 copy-done.5
  41.2 5.3 %boundary1.1 = (f32[1024,512]{1,0:T(8,128)S(1)}, bf16[4,512,256]{2,1,0:T(8,128)(2,1)S(1)}, f32[288,128]{1,0:T(8,128)S(1)}) custom-call(s32[1]{0:T(128)S(6)} %copy.21.refs_0_, f32[288,128]{1,0:T(8,128)S(1)} %bitcast.24, bf16[1024,512]{1,0:T(8,128)(2,1)S(1)} %get-tuple-element.30.refs_2_, bf16[4,512,256]{2,1,0:T(8,128)(2,1)S(1)} %get-tuple-element.31.refs_3_, ...), custom_call_target="tpu_custom_call" | custom-call | tf_op jit(solution)/shard_map/boundary1/pallas_call | solution.py:297
  46.6 13.9 %all_to_all.42 = f32[32,1,1152]{2,1,0:T(1,128)S(1)} all-to-all(f32[32,1,1152]{2,1,0:T(1,128)S(1)} %bitcast.30), channel_id=1, replica_groups=mesh['batch'=8,'pts'=32] {'pts'}, dimensions={0} | all-to-all | bytes 294912 | tf_op jit(solution)/shard_map/all_to_all | solution.py:318
  60.5 13.7 %all_to_all.43 = f32[32,1,1152]{2,1,0:T(1,128)S(1)} all-to-all(f32[32,1,1152]{2,1,0:T(1,128)S(1)} %bitcast.19), channel_id=1, replica_groups=mesh['batch'=8,'pts'=32] {'pts'}, dimensions={0} | all-to-all | bytes 294912 | tf_op jit(solution)/shard_map/all_to_all | solution.py:328
  74.3 5.3 %boundary2.1 = (f32[1024,512]{1,0:T(8,128)S(1)}, bf16[4,512,256]{2,1,0:T(8,128)(2,1)S(1)}, f32[288,128]{1,0:T(8,128)S(1)}) custom-call(s32[1]{0:T(128)S(6)} %copy.21.refs_0_, f32[288,128]{1,0:T(8,128)S(1)} %bitcast.27, f32[1024,512]{1,0:T(8,128)S(1)} %get-tuple-element.43.refs_2_, bf16[4,512,256]{2,1,0:T(8,128)(2,1)S(1)} %get-tuple-element.44.refs_3_, ...), custom_call_target="tpu_custom_call" | custom-call | tf_op jit(solution)/shard_map/boundary2/pallas_call | solution.py:297
  79.6 14.0 %all_to_all.44 = f32[32,1,1152]{2,1,0:T(1,128)S(1)} all-to-all(f32[32,1,1152]{2,1,0:T(1,128)S(1)} %bitcast.31), channel_id=1, replica_groups=mesh['batch'=8,'pts'=32] {'pts'}, dimensions={0} | all-to-all | bytes 294912 | tf_op jit(solution)/shard_map/all_to_all | solution.py:318
  93.6 14.0 %all_to_all.45 = f32[32,1,1152]{2,1,0:T(1,128)S(1)} all-to-all(f32[32,1,1152]{2,1,0:T(1,128)S(1)} %bitcast.21), channel_id=1, replica_groups=mesh['batch'=8,'pts'=32] {'pts'}, dimensions={0} | all-to-all | bytes 294912 | tf_op jit(solution)/shard_map/all_to_all | solution.py:328
  107.6 5.3 %boundary3.1 = (f32[1024,512]{1,0:T(8,128)S(1)}, bf16[4,512,256]{2,1,0:T(8,128)(2,1)S(1)}, f32[288,128]{1,0:T(8,128)S(1)}) custom-call(s32[1]{0:T(128)S(6)} %copy.21.refs_0_, f32[288,128]{1,0:T(8,128)S(1)} %bitcast.26, f32[1024,512]{1,0:T(8,128)S(1)} %get-tuple-element.46.refs_2_, bf16[4,512,256]{2,1,0:T(8,128)(2,1)S(1)} %get-tuple-element.47.refs_3_, ...), custom_call_target="tpu_custom_call" | custom-call | tf_op jit(solution)/shard_map/boundary3/pallas_call | solution.py:297
  112.9 14.1 %all_to_all.46 = f32[32,1,1152]{2,1,0:T(1,128)S(1)} all-to-all(f32[32,1,1152]{2,1,0:T(1,128)S(1)} %bitcast.28), channel_id=1, replica_groups=mesh['batch'=8,'pts'=32] {'pts'}, dimensions={0} | all-to-all | bytes 294912 | tf_op jit(solution)/shard_map/all_to_all | solution.py:318
  127.0 13.9 %all_to_all.47 = f32[32,1,1152]{2,1,0:T(1,128)S(1)} all-to-all(f32[32,1,1152]{2,1,0:T(1,128)S(1)} %bitcast.23), channel_id=1, replica_groups=mesh['batch'=8,'pts'=32] {'pts'}, dimensions={0} | all-to-all | bytes 294912 | tf_op jit(solution)/shard_map/all_to_all | solution.py:328
  140.9 4.1 %boundary4.1 = bf16[1024,512]{1,0:T(8,128)(2,1)} custom-call(s32[1]{0:T(128)S(6)} %copy.21.refs_0_, f32[288,128]{1,0:T(8,128)S(1)} %bitcast.25, f32[1024,512]{1,0:T(8,128)S(1)} %get-tuple-element.49.refs_2_, bf16[4,512,256]{2,1,0:T(8,128)(2,1)S(1)} %get-tuple-element.50.refs_3_, bf16[4,64,64]{2,1,0:T(8,128)(2,1)S(1)} %copy-done.3, ...), custom_call_target="tpu_custom_call" | custom-call | tf_op jit(solution)/shard_map/boundary4/pallas_call | solution.py:297
  (4 shorter events, 0.1 us)
Async XLA Ops:
  0.7 40.6 %copy-start = (bf16[4,512,512]{2,1,0:T(8,128)(2,1)S(1)}, bf16[4,512,512]{2,1,0:T(8,128)(2,1)}, u32[]{:S(2)}) copy-start(bf16[4,512,512]{2,1,0:T(8,128)(2,1)} %refs_11_.2) | copy-start | bytes 6291460
  0.7 40.5 %copy-start.1 = (bf16[4,512,512]{2,1,0:T(8,128)(2,1)S(1)}, bf16[4,512,512]{2,1,0:T(8,128)(2,1)}, u32[]{:S(2)}) copy-start(bf16[4,512,512]{2,1,0:T(8,128)(2,1)} %refs_12_.2) | copy-start | bytes 6291460
  0.7 40.5 %copy-start.2 = (bf16[4,512,512]{2,1,0:T(8,128)(2,1)S(1)}, bf16[4,512,512]{2,1,0:T(8,128)(2,1)}, u32[]{:S(2)}) copy-start(bf16[4,512,512]{2,1,0:T(8,128)(2,1)} %refs_7_.5) | copy-start | bytes 6291460
  0.7 40.5 %copy-start.3 = (bf16[4,64,64]{2,1,0:T(8,128)(2,1)S(1)}, bf16[4,64,64]{2,1,0:T(8,128)(2,1)}, u32[]{:S(2)}) copy-start(bf16[4,64,64]{2,1,0:T(8,128)(2,1)} %refs_4_.5) | copy-start | bytes 98308
  0.7 40.5 %copy-start.4 = (bf16[4,64,64]{2,1,0:T(8,128)(2,1)S(1)}, bf16[4,64,64]{2,1,0:T(8,128)(2,1)}, u32[]{:S(2)}) copy-start(bf16[4,64,64]{2,1,0:T(8,128)(2,1)} %refs_5_.5) | copy-start | bytes 98308
  0.7 40.5 %copy-start.5 = (bf16[4,64,64]{2,1,0:T(8,128)(2,1)S(1)}, bf16[4,64,64]{2,1,0:T(8,128)(2,1)}, u32[]{:S(2)}) copy-start(bf16[4,64,64]{2,1,0:T(8,128)(2,1)} %refs_6_.5) | copy-start | bytes 98308
